TPU v7x, 32 devices: a whole 2x2x4 slice. The times are simulated.
32 devices in a mesh: seq: 16 (over z, y, x), head: 2 (over core).
Axes of the slice: x: 2, y: 2, z: 4, core: 2. Of those that a mesh axis runs over, the one named last changes fastest.
Arguments:
- queries: bfloat16 [4096, 32, 128], P('seq', 'head'), may hold values from -192 to 192
- keys: bfloat16 [4096, 8, 128], P(('seq', 'head')), may hold values from -6 to 6
- values: bfloat16 [4096, 8, 128], P(('seq', 'head')), may hold values from -6 to 6
- doc_start: int32 [4096], P('seq'), may hold values from 0 to 4095, as said below
- tile_list: int32 [16, 18], P('seq'), may hold values from 0 to 31, as said below
- tile_count: int32 [16], P('seq'), may hold values from 2 to 18, as said below
Outputs:
- attention_out: bfloat16 [4096, 32, 128], P('seq', 'head')
Inputs may be any that keep to these rules, and one draw needn't show every extreme that they name: doc_start never falls, doc_start[i] <= i, and a new document begins at each position where it changes; documents hold 1 to 2048 tokens, one exactly 2048. `tile_list`: row s holds in its first tile_count[s] entries, ascending, exactly the tiles (tile t holds key positions t * 128 to t * 128 + 127) that contain a key visible to some query of positions s * 256 to s * 256 + 255; the later entries equal s * 2. `tile_count`: some row reaches 18.
All inputs are finite; a program needn't handle non-finite values.
Results may differ from a plain program's by a relative error of at most 0.004.
Values may be sent and summed in bfloat16 or wider, within the bound.
A program may use at most 64 MiB of HBM per device.

v0:
```python
import functools

import jax
import jax.numpy as jnp
from jax import lax
from jax.experimental import pallas as pl
from jax.experimental.pallas import tpu as pltpu
from jax.sharding import PartitionSpec as P

TILE = 128
MAXDOC = 2048
PLANE = 4
LOG2E = 1.4426950408889634
NEGATIVE = -1e30
FAR = 1 << 24


def kernel(groups, levels, rel_ref, q_ref, k_ref, v_ref, o_ref, kbuf, vbuf, top, total, acc,
           local_sem, partner_send, own_send, relay_send, recv):
    me = lax.axis_index("seq")
    core = lax.axis_index("head")
    z, p = me // PLANE, me % PLANE
    side = p % 2
    px = p + 1 - 2 * side
    py = p + 2 - 4 * (p // 2)
    pd = PLANE - 1 - p
    base = z * PLANE
    last = groups - 1
    heads = kbuf.shape[1]
    q_heads = q_ref.shape[0]
    group_size = q_heads // heads
    tile = k_ref.shape[1]
    tokens = kbuf.shape[2]
    scale = LOG2E * q_ref.shape[-1] ** (-0.5)
    residue = {"own": p, "x": px, "y": py, "diag": pd}
    bufs = (kbuf, vbuf)

    def where_to(seq):
        return {"seq": seq, "head": core}

    barrier = pltpu.get_barrier_semaphore()
    pl.semaphore_signal(barrier, inc=1, device_id={"seq": me, "head": 1 - core},
                        device_id_type=pl.DeviceIdType.MESH)
    for mate in (px, py):
        pl.semaphore_signal(barrier, inc=1, device_id=where_to(base + mate),
                            device_id_type=pl.DeviceIdType.MESH)

    @pl.when(z < last)
    def _():
        pl.semaphore_signal(barrier, inc=1, device_id=where_to(me + PLANE),
                            device_id_type=pl.DeviceIdType.MESH)

    @pl.when(z > 0)
    def _():
        pl.semaphore_signal(barrier, inc=1, device_id=where_to(me - PLANE),
                            device_id_type=pl.DeviceIdType.MESH)

    pl.semaphore_wait(barrier, 3 + jnp.minimum(last - z, 1) + jnp.minimum(z, 1))

    mine = pl.multiple_of(core * tile, tile)
    theirs = pl.multiple_of((1 - core) * tile, tile)
    first_slot = p
    own_parts = (
        (k_ref, kbuf.at[first_slot, :, pl.ds(mine, tile), :]),
        (v_ref, vbuf.at[first_slot, :, :, pl.ds(mine, tile)]),
    )
    partner = []
    local = []
    for which in range(2):
        src, dst = own_parts[which]
        copy = pltpu.make_async_remote_copy(
            src_ref=src.at[pl.ds((1 - core) * heads, heads)],
            dst_ref=dst,
            send_sem=partner_send.at[which],
            recv_sem=recv.at[which, first_slot],
            device_id={"seq": me, "head": 1 - core},
            device_id_type=pl.DeviceIdType.MESH,
        )
        copy.start()
        partner.append(copy)
        copy = pltpu.make_async_copy(src.at[pl.ds(core * heads, heads)], dst, local_sem.at[which])
        copy.start()
        local.append(copy)

    def needs(level, r, dst):
        if level == 0:
            return r < dst
        if level == levels:
            return r > dst
        return dst >= 0

    pending = []

    def send(condition, which, level, r, to_level, seq, sem):
        copy = pltpu.make_async_remote_copy(
            src_ref=bufs[which].at[level * PLANE + r],
            dst_ref=bufs[which].at[to_level * PLANE + r],
            send_sem=sem,
            recv_sem=recv.at[which, to_level * PLANE + r],
            device_id=where_to(seq),
            device_id_type=pl.DeviceIdType.MESH,
        )
        pl.when(condition)(copy.start)
        pending.append((condition, copy))

    def have(level, origin):
        held = z >= level
        if origin != "own":
            held = held & needs(level, residue[origin], p)
        return held

    def arrive(level, origin, which):
        r = residue[origin]
        slot = level * PLANE + r
        here = have(level, origin)

        if level == 0 and origin == "own":
            partner[which].wait_recv()
            local[which].wait()
        else:
            @pl.when(here)
            def _():
                pltpu.make_async_remote_copy(
                    src_ref=bufs[which].at[slot],
                    dst_ref=bufs[which].at[slot],
                    send_sem=own_send.at[0, 0, 0],
                    recv_sem=recv.at[which, slot],
                    device_id=where_to(base + px),
                    device_id_type=pl.DeviceIdType.MESH,
                ).wait_recv()

        if origin == "own":
            if level < levels:
                send(here & (z < last), which, level, r, level + 1, me + PLANE, own_send.at[0, level, which])
            send(here & needs(level, p, px), which, level, r, level, base + px, own_send.at[1, level, which])
            send(here & needs(level, p, py), which, level, r, level, base + py, own_send.at[2, level, which])
        elif origin == "x":
            if which == 1:
                go = here & needs(level, px, py)
                if level in (0, levels):
                    go = go & ((px == 0) | (px == PLANE - 1))
                send(go, which, level, r, level, base + py, relay_send.at[0, level, which])
        elif origin == "y":
            go = here & needs(level, py, px)
            if which == 1:
                if level in (0, levels):
                    go = go & (py != 0) & (py != PLANE - 1)
                else:
                    go = None
            if go is not None:
                send(go, which, level, r, level, base + px, relay_send.at[1, level, which])

    def mask_of(slot, causal):
        keys = lax.broadcasted_iota(jnp.int32, (tile, tokens), 0)
        parts = []
        for half in range(tokens // tile):
            part = keys >= rel_ref[pl.ds(slot * (tokens // tile) + half, 1), :]
            if causal:
                part = part & (keys + half * tile <= lax.broadcasted_iota(jnp.int32, (tile, tokens), 1))
            parts.append(part)
        return jnp.concatenate([jnp.where(part, 0.0, NEGATIVE) for part in parts], axis=0)

    def compute(slot, first):
        def one_head(g, _):
            k_tile = kbuf[slot, g]
            v_tile = vbuf[slot, g]
            bias = mask_of(slot, first)
            for c in range(group_size):
                h = g * group_size + c
                scores = lax.dot_general(k_tile, q_ref[h], (((1,), (1,)), ((), ())),
                                         preferred_element_type=jnp.float32)
                scores = scores + bias
                new_top = jnp.max(scores, axis=0, keepdims=True)
                if not first:
                    old_top = top[h]
                    new_top = jnp.maximum(old_top, new_top)
                    factor = jnp.exp2((old_top - new_top) * scale)
                weights = jnp.exp2((scores - new_top) * scale)
                weight_sum = jnp.sum(weights, axis=0, keepdims=True)
                summed = lax.dot_general(v_tile, weights.astype(jnp.bfloat16), (((1,), (0,)), ((), ())),
                                         preferred_element_type=jnp.float32)
                top[h] = new_top
                if first:
                    total[h] = weight_sum
                    acc[h] = summed
                else:
                    total[h] = total[h] * factor + weight_sum
                    acc[h] = acc[h] * factor + summed
            return 0

        lax.fori_loop(0, heads, one_head, 0)

    stages = [[(0, "own")], [(1, "own"), (0, "x"), (0, "y")]]
    stages.append([(0, "diag"), (1, "x"), (1, "y"), (2, "own")])
    stages.append([(1, "diag"), (2, "x"), (2, "y")])
    stages.append([(2, "diag")])
    for stage in stages:
        for which in range(2):
            for level, origin in stage:
                arrive(level, origin, which)
        for level, origin in stage:
            slot = level * PLANE + residue[origin]
            if level == 0 and origin == "own":
                compute(slot, True)
            else:
                pl.when(have(level, origin))(functools.partial(compute, slot, False))

    def finish(h, _):
        o_ref[h] = jnp.transpose(acc[h] / total[h]).astype(o_ref.dtype)
        return 0

    lax.fori_loop(0, q_heads, finish, 0)
    for copy in partner:
        copy.wait_send()
    for condition, copy in pending:
        pl.when(condition)(copy.wait_send)


def body(groups, queries, keys, values, doc_start, tile_list, tile_count):
    tokens, q_heads, dim = queries.shape
    tile, all_heads, _ = keys.shape
    heads = all_heads // lax.axis_size("head")
    levels = MAXDOC // tokens // PLANE
    slots = (levels + 1) * PLANE
    halves = tokens // tile
    z = lax.axis_index("seq") // PLANE
    slot = jnp.arange(slots, dtype=jnp.int32)
    block = (z - slot // PLANE) * PLANE + slot % PLANE
    ids = (block[:, None] * halves + jnp.arange(halves, dtype=jnp.int32)).reshape(-1)
    live = jnp.arange(tile_list.shape[1], dtype=jnp.int32) < tile_count[0]
    listed = jnp.any((tile_list[0][None, :] == ids[:, None]) & live[None, :], axis=1)
    rel = jnp.where(listed[:, None], doc_start[None, :] - ids[:, None] * tile, FAR)

    vmem = pl.BlockSpec(memory_space=pltpu.VMEM)
    out = pl.pallas_call(
        functools.partial(kernel, groups, levels),
        out_shape=jax.ShapeDtypeStruct((q_heads, tokens, dim), queries.dtype),
        in_specs=[vmem] * 4,
        out_specs=vmem,
        scratch_shapes=[
            pltpu.VMEM((slots, heads, tokens, dim), keys.dtype),
            pltpu.VMEM((slots, heads, dim, tokens), values.dtype),
            pltpu.VMEM((q_heads, 1, tokens), jnp.float32),
            pltpu.VMEM((q_heads, 1, tokens), jnp.float32),
            pltpu.VMEM((q_heads, dim, tokens), jnp.float32),
            pltpu.SemaphoreType.DMA((2,)),
            pltpu.SemaphoreType.DMA((2,)),
            pltpu.SemaphoreType.DMA((3, levels + 1, 2)),
            pltpu.SemaphoreType.DMA((2, levels + 1, 2)),
            pltpu.SemaphoreType.DMA((2, slots)),
        ],
        compiler_params=pltpu.CompilerParams(
            collective_id=0, has_side_effects=True, vmem_limit_bytes=40 * 1024 * 1024),
    )(rel, queries.transpose(1, 0, 2), keys.transpose(1, 0, 2), values.transpose(1, 2, 0))
    return out.transpose(1, 0, 2)


def solution(mesh):
    in_specs = (
        P("seq", "head", None),
        P(("seq", "head"), None, None),
        P(("seq", "head"), None, None),
        P("seq"),
        P("seq", None),
        P("seq"),
    )
    return jax.shard_map(
        functools.partial(body, mesh.shape["seq"] // PLANE),
        mesh=mesh, in_specs=in_specs, out_specs=P("seq", "head", None), check_vma=False)
```

profile of v0, /device:TPU:17, one launch (start us, length us, event | category | flops | bytes accessed | tf_op | source)
XLA Modules:
  0.0 77.7 jit_solution(16413141504816214677)
XLA Ops:
  0.0 0.0 copy-start
  0.8 0.1 iota_add_fusion
  0.8 0.1 add.52
  0.9 0.8 %and_reduce_fusion = pred[24]{0:T(512)(128)(4,1)S(1)} fusion(s32[18]{0:T(128)} %bitcast.15, s32[24]{0:T(128)S(1)} %add.52, pred[18]{0:T(512)(128)(4,1)S(1)} %iota_compare_fusion), kind=kLoop, calls=%fused_computation.3 | loop fusion | flops 1272 | bytes 210 | tf_op jit(solution)/shard_map/reduce_or | solution.py:231
  1.8 0.8 subtract_select_fusion.rel_ref
  2.5 1.0 %copy.22 = bf16[128,8,128]{2,0,1:T(8,128)(2,1)S(1)} copy(bf16[128,8,128]{2,1,0:T(8,128)(2,1)} %param.7) | data formatting | bytes 524288 | tf_op args[1]
  3.5 1.2 %copy.17 = bf16[128,8,128]{0,2,1:T(8,128)(2,1)S(1)} copy(bf16[128,8,128]{2,1,0:T(8,128)(2,1)} %param.8) | data formatting | bytes 524288 | tf_op args[2]
  4.7 0.0 copy-done
  4.7 0.3 copy.21
  5.0 71.0 %shard_map.64 = bf16[16,256,128]{2,1,0:T(8,128)(2,1)S(1)} custom-call(s32[24,256]{1,0:T(8,128)S(1)} %subtract_select_fusion.rel_ref, bf16[16,256,128]{2,1,0:T(8,128)(2,1)S(1)} %bitcast.12, bf16[8,128,128]{2,1,0:T(8,128)(2,1)S(1)} %bitcast.13, bf16[8,128,128]{2,1,0:T(8,128)(2,1)S(1)} %bitcast.14), custom_call_target="tpu_custom_call" | custom-call | tf_op jit(solution)/shard_map/pallas_call | solution.py:235
  76.0 1.6 %copy.18 = bf16[256,16,128]{2,1,0:T(8,128)(2,1)} copy(bf16[256,16,128]{2,0,1:T(8,128)(2,1)S(1)} %bitcast.11) | data formatting | bytes 2097152 | tf_op jit(solution)/shard_map/transpose | solution.py:255
  (3 shorter events, 0.0 us)
Async XLA Ops:
  0.0 4.7 %copy-start = (bf16[256,16,128]{2,1,0:T(8,128)(2,1)S(1)}, bf16[256,16,128]{2,1,0:T(8,128)(2,1)}, u32[]{:S(2)}) copy-start(bf16[256,16,128]{2,1,0:T(8,128)(2,1)} %param.6) | copy-start | bytes 3145732
where the time goes:
time: 78.2 us; the launch traced here: 77.7 us
  Pallas kernels  71 us (91%)
  local copies, waits for them, and re-layouts  4.15 us (5%)
  other arithmetic  1.68 us (2%)
  between operations  0.79 us (1%)
    pallas_call x1, Pallas kernels, body(): pl.pallas_call(functools.partial(kernel, groups, levels), out_shape=jax.S...  71 us
    unnamed x5, local copies, waits for them, and re-layouts  2.42 us
    transpose x1, local copies, waits for them, and re-layouts, body(): return out.transpose(1, 0, 2)  1.65 us

commit v1 on v0

v1 whole, which is shorter than its diff:
```python
import functools

import jax
import jax.numpy as jnp
from jax import lax
from jax.experimental import pallas as pl
from jax.experimental.pallas import tpu as pltpu
from jax.sharding import PartitionSpec as P

TILE = 128
MAXDOC = 2048
PLANE = 4
LOG2E = 1.4426950408889634
NEGATIVE = -1e30
FAR = 1 << 24


def kernel(groups, levels, rel_ref, q_ref, kv_ref, o_ref, buf, top, total, acc,
           local_sem, partner_send, own_send, relay_send, recv):
    me = lax.axis_index("seq")
    core = lax.axis_index("head")
    z, p = me // PLANE, me % PLANE
    side = p % 2
    px = p + 1 - 2 * side
    py = p + 2 - 4 * (p // 2)
    pd = PLANE - 1 - p
    base = z * PLANE
    last = groups - 1
    heads = buf.shape[1]
    q_heads = q_ref.shape[0]
    group_size = q_heads // heads
    tile = kv_ref.shape[2]
    tokens = buf.shape[3]
    scale = LOG2E * q_ref.shape[-1] ** (-0.5)
    residue = {"own": p, "x": px, "y": py, "diag": pd}
    split = heads // 2

    def where_to(seq):
        return {"seq": seq, "head": core}

    barrier = pltpu.get_barrier_semaphore()
    pl.semaphore_signal(barrier, inc=1, device_id={"seq": me, "head": 1 - core},
                        device_id_type=pl.DeviceIdType.MESH)
    for mate in (px, py):
        pl.semaphore_signal(barrier, inc=1, device_id=where_to(base + mate),
                            device_id_type=pl.DeviceIdType.MESH)

    @pl.when(z < last)
    def _():
        pl.semaphore_signal(barrier, inc=1, device_id=where_to(me + PLANE),
                            device_id_type=pl.DeviceIdType.MESH)

    @pl.when(z > 0)
    def _():
        pl.semaphore_signal(barrier, inc=1, device_id=where_to(me - PLANE),
                            device_id_type=pl.DeviceIdType.MESH)

    pl.semaphore_wait(barrier, 3 + jnp.minimum(last - z, 1) + jnp.minimum(z, 1))

    mine = pl.multiple_of(core * tile, tile)
    own_part = buf.at[p, :, :, pl.ds(mine, tile), :]
    partner = pltpu.make_async_remote_copy(
        src_ref=kv_ref.at[pl.ds((1 - core) * heads, heads)],
        dst_ref=own_part,
        send_sem=partner_send,
        recv_sem=recv.at[p, 0],
        device_id={"seq": me, "head": 1 - core},
        device_id_type=pl.DeviceIdType.MESH,
    )
    partner.start()
    local = pltpu.make_async_copy(kv_ref.at[pl.ds(core * heads, heads)], own_part, local_sem)
    local.start()

    def needs(level, r, dst):
        if level == 0:
            return r < dst
        if level == levels:
            return r > dst
        return dst >= 0

    def sends(level, origin, g):
        r = residue[origin]
        slot = level * PLANE + r
        here = have(level, origin)

        def copy(to_level, seq, sem):
            return pltpu.make_async_remote_copy(
                src_ref=buf.at[slot, g],
                dst_ref=buf.at[to_level * PLANE + r, g],
                send_sem=sem,
                recv_sem=recv.at[to_level * PLANE + r, g],
                device_id=where_to(seq),
                device_id_type=pl.DeviceIdType.MESH,
            )

        found = []
        if origin == "own":
            if level < levels:
                found.append((here & (z < last), copy(level + 1, me + PLANE, own_send.at[0, level, g])))
            found.append((here & needs(level, p, px), copy(level, base + px, own_send.at[1, level, g])))
            found.append((here & needs(level, p, py), copy(level, base + py, own_send.at[2, level, g])))
        elif origin == "x":
            go = here & needs(level, px, py) & (g >= split)
            if level in (0, levels):
                go = go & ((px == 0) | (px == PLANE - 1))
            found.append((go, copy(level, base + py, relay_send.at[0, level, g])))
        elif origin == "y":
            go = here & needs(level, py, px)
            if level in (0, levels):
                go = go & ((g < split) | ((py != 0) & (py != PLANE - 1)))
            else:
                go = go & (g < split)
            found.append((go, copy(level, base + px, relay_send.at[1, level, g])))
        return found

    def have(level, origin):
        held = z >= level
        if origin != "own":
            held = held & needs(level, residue[origin], p)
        return held

    def arrive(level, origin, g):
        if (level, origin) != (0, "own"):
            slot = level * PLANE + residue[origin]

            @pl.when(have(level, origin))
            def _():
                pltpu.make_async_remote_copy(
                    src_ref=buf.at[slot, g],
                    dst_ref=buf.at[slot, g],
                    send_sem=own_send.at[0, 0, 0],
                    recv_sem=recv.at[slot, g],
                    device_id=where_to(base + px),
                    device_id_type=pl.DeviceIdType.MESH,
                ).wait_recv()

        for condition, copy in sends(level, origin, g):
            pl.when(condition)(copy.start)

    def mask_of(slot, causal):
        keys = lax.broadcasted_iota(jnp.int32, (tile, tokens), 0)
        parts = []
        for half in range(tokens // tile):
            part = keys >= rel_ref[pl.ds(slot * (tokens // tile) + half, 1), :]
            if causal:
                part = part & (keys + half * tile <= lax.broadcasted_iota(jnp.int32, (tile, tokens), 1))
            parts.append(part)
        return jnp.concatenate([jnp.where(part, 0.0, NEGATIVE) for part in parts], axis=0)

    def compute(slot, g, first):
        k_tile = buf[slot, g, 0]
        v_tile = jnp.concatenate(
            [buf[slot, g, 1, half * tile:(half + 1) * tile] for half in range(tokens // tile)], axis=1)
        bias = mask_of(slot, first)
        for c in range(group_size):
            h = g * group_size + c
            scores = lax.dot_general(k_tile, q_ref[h], (((1,), (1,)), ((), ())),
                                     preferred_element_type=jnp.float32)
            scores = scores + bias
            new_top = jnp.max(scores, axis=0, keepdims=True)
            if not first:
                old_top = top[h]
                new_top = jnp.maximum(old_top, new_top)
                factor = jnp.exp2((old_top - new_top) * scale)
            weights = jnp.exp2((scores - new_top) * scale)
            weight_sum = jnp.sum(weights, axis=0, keepdims=True)
            summed = lax.dot_general(v_tile, weights.astype(jnp.bfloat16), (((1,), (0,)), ((), ())),
                                     preferred_element_type=jnp.float32)
            top[h] = new_top
            if first:
                total[h] = weight_sum
                acc[h] = summed
            else:
                total[h] = total[h] * factor + weight_sum
                acc[h] = acc[h] * factor + summed

    partner.wait_recv()
    local.wait()
    stages = [
        [(0, "own")],
        [(1, "own"), (0, "x"), (0, "y")],
        [(1, "x"), (1, "y"), (0, "diag"), (2, "own")],
        [(1, "diag"), (2, "x"), (2, "y")],
        [(2, "diag")],
    ]
    everything = [entry for stage in stages for entry in stage]

    def start_own(g, _):
        arrive(0, "own", g)
        return 0

    lax.fori_loop(0, heads, start_own, 0)
    for stage in stages:
        def one_head(g, _):
            for level, origin in stage:
                slot = level * PLANE + residue[origin]
                if (level, origin) == (0, "own"):
                    compute(slot, g, True)
            if stage[0] != (0, "own"):
                for level, origin in stage:
                    arrive(level, origin, g)
                for level, origin in stage:
                    slot = level * PLANE + residue[origin]
                    pl.when(have(level, origin))(functools.partial(compute, slot, g, False))
            return 0

        lax.fori_loop(0, heads, one_head, 0)

    def finish(h, _):
        o_ref[h] = jnp.transpose(acc[h] / total[h]).astype(o_ref.dtype)
        return 0

    lax.fori_loop(0, q_heads, finish, 0)
    partner.wait_send()

    def sent(g, _):
        for level, origin in everything:
            for condition, copy in sends(level, origin, g):
                pl.when(condition)(copy.wait_send)
        return 0

    lax.fori_loop(0, heads, sent, 0)


def body(groups, queries, keys, values, doc_start, tile_list, tile_count):
    tokens, q_heads, dim = queries.shape
    tile, all_heads, _ = keys.shape
    heads = all_heads // lax.axis_size("head")
    levels = MAXDOC // tokens // PLANE
    slots = (levels + 1) * PLANE
    halves = tokens // tile
    z = lax.axis_index("seq") // PLANE
    slot = jnp.arange(slots, dtype=jnp.int32)
    block = (z - slot // PLANE) * PLANE + slot % PLANE
    ids = (block[:, None] * halves + jnp.arange(halves, dtype=jnp.int32)).reshape(-1)
    live = jnp.arange(tile_list.shape[1], dtype=jnp.int32) < tile_count[0]
    listed = jnp.any((tile_list[0][None, :] == ids[:, None]) & live[None, :], axis=1)
    rel = jnp.where(listed[:, None], doc_start[None, :] - ids[:, None] * tile, FAR)

    vmem = pl.BlockSpec(memory_space=pltpu.VMEM)
    out = pl.pallas_call(
        functools.partial(kernel, groups, levels),
        out_shape=jax.ShapeDtypeStruct((q_heads, tokens, dim), queries.dtype),
        in_specs=[vmem] * 3,
        out_specs=vmem,
        scratch_shapes=[
            pltpu.VMEM((slots, heads, 2, tokens, dim), keys.dtype),
            pltpu.VMEM((q_heads, 1, tokens), jnp.float32),
            pltpu.VMEM((q_heads, 1, tokens), jnp.float32),
            pltpu.VMEM((q_heads, dim, tokens), jnp.float32),
            pltpu.SemaphoreType.DMA,
            pltpu.SemaphoreType.DMA,
            pltpu.SemaphoreType.DMA((3, levels + 1, heads)),
            pltpu.SemaphoreType.DMA((2, levels + 1, heads)),
            pltpu.SemaphoreType.DMA((slots, heads)),
        ],
        compiler_params=pltpu.CompilerParams(
            collective_id=0, has_side_effects=True, vmem_limit_bytes=40 * 1024 * 1024),
    )(rel, queries.transpose(1, 0, 2), jnp.stack([keys.transpose(1, 0, 2), values.transpose(1, 2, 0)], axis=1))
    return out.transpose(1, 0, 2)


def solution(mesh):
    in_specs = (
        P("seq", "head", None),
        P(("seq", "head"), None, None),
        P(("seq", "head"), None, None),
        P("seq"),
        P("seq", None),
        P("seq"),
    )
    return jax.shard_map(
        functools.partial(body, mesh.shape["seq"] // PLANE),
        mesh=mesh, in_specs=in_specs, out_specs=P("seq", "head", None), check_vma=False)
```

time: 78.2 us -> 65.8 us (0.84)
  Pallas kernels: 71 us -> 59.9 us
  other arithmetic: 1.68 us -> 0.4 us
    pallas_call x1, Pallas kernels: 71 us -> 59.9 us  [body(): pl.pallas_call(functools.partial(kernel, groups, levels), out_shape=jax.S...]
    unnamed x5 -> x11, local copies, waits for them, and re-layouts: 2.42 us -> 2.82 us
where the time goes in v1:
time: 65.8 us; the launch traced here: 65.6 us
  Pallas kernels  59.9 us (91%)
  local copies, waits for them, and re-layouts  4.55 us (7%)
  between operations  0.73 us (1%)
    pallas_call x1, Pallas kernels, body(): pl.pallas_call(functools.partial(kernel, groups, levels), out_shape=jax.S...  59.9 us
    unnamed x11, local copies, waits for them, and re-layouts  2.82 us
    transpose x1, local copies, waits for them, and re-layouts, body(): return out.transpose(1, 0, 2)  1.65 us

profile of v1, /device:TPU:17, one launch (start us, length us, event | category | flops | bytes accessed | tf_op | source)
XLA Modules:
  0.0 65.6 jit_solution(6839469001515654904)
XLA Ops:
  0.7 0.1 iota_add_fusion
  0.7 0.0 copy-start.3
  0.8 0.1 add.52
  0.8 0.6 copy-done.3
  1.4 0.2 and_reduce_fusion
  1.6 0.0 copy-start.2
  1.6 0.7 %copy-done.2 = s32[256]{0:T(256)S(1)} copy-done((s32[256]{0:T(256)S(1)}, s32[256]{0:T(256)}, u32[]{:S(2)}) %copy-start.2) | copy-done | bytes 1048
  2.3 0.0 copy-start.1
  2.3 0.1 subtract_select_fusion.rel_ref
  2.3 0.0 copy-start
  2.4 1.1 %copy.22 = bf16[128,8,128]{2,0,1:T(8,128)(2,1)S(1)} copy(bf16[128,8,128]{2,1,0:T(8,128)(2,1)} %param.7) | data formatting | bytes 524288 | tf_op args[1]
  3.4 0.0 copy-done.1
  3.4 0.2 copy.17
  3.7 0.1 pad_maximum_fusion.kv_ref
  3.7 0.0 copy-done
  3.7 0.3 copy.21
  4.0 59.9 %shard_map.64 = bf16[16,256,128]{2,1,0:T(8,128)(2,1)S(1)} custom-call(s32[24,256]{1,0:T(8,128)S(1)} %subtract_select_fusion.rel_ref, bf16[16,256,128]{2,1,0:T(8,128)(2,1)S(1)} %bitcast.16, bf16[8,2,128,128]{3,2,1,0:T(8,128)(2,1)S(1)} %pad_maximum_fusion.kv_ref), custom_call_target="tpu_custom_call" | custom-call | tf_op jit(solution)/shard_map/pallas_call | solution.py:241
  64.0 1.6 %copy.18 = bf16[256,16,128]{2,1,0:T(8,128)(2,1)} copy(bf16[256,16,128]{2,0,1:T(8,128)(2,1)S(1)} %bitcast.15) | data formatting | bytes 2097152 | tf_op jit(solution)/shard_map/transpose | solution.py:260
  (3 shorter events, 0.0 us)
Async XLA Ops:
  0.7 0.7 %copy-start.3 = (s32[1,18]{1,0:T(1,128)S(1)}, s32[1,18]{1,0:T(1,128)}, u32[]{:S(2)}) copy-start(s32[1,18]{1,0:T(1,128)} %param.10) | copy-start | bytes 220
  1.6 0.7 %copy-start.2 = (s32[256]{0:T(256)S(1)}, s32[256]{0:T(256)}, u32[]{:S(2)}) copy-start(s32[256]{0:T(256)} %param.9) | copy-start | bytes 3076
  2.3 1.2 %copy-start.1 = (bf16[128,8,128]{2,1,0:T(8,128)(2,1)S(1)}, bf16[128,8,128]{2,1,0:T(8,128)(2,1)}, u32[]{:S(2)}) copy-start(bf16[128,8,128]{2,1,0:T(8,128)(2,1)} %param.8) | copy-start | bytes 786436
  2.3 1.4 %copy-start = (bf16[256,16,128]{2,1,0:T(8,128)(2,1)S(1)}, bf16[256,16,128]{2,1,0:T(8,128)(2,1)}, u32[]{:S(2)}) copy-start(bf16[256,16,128]{2,1,0:T(8,128)(2,1)} %param.6) | copy-start | bytes 3145732

commit v2 on v1

--- a/solution.py
+++ b/solution.py
@@ -199,7 +199,6 @@
             if stage[0] != (0, "own"):
                 for level, origin in stage:
                     arrive(level, origin, g)
-                for level, origin in stage:
                     slot = level * PLANE + residue[origin]
                     pl.when(have(level, origin))(functools.partial(compute, slot, g, False))
             return 0

time: 65.8 us -> 65.6 us (level)
  no operation moved by 1% of the time
where the time goes in v2:
time: 65.6 us; the launch traced here: 65.5 us
  Pallas kernels  59.8 us (91%)
  local copies, waits for them, and re-layouts  4.55 us (7%)
  between operations  0.73 us (1%)
    pallas_call x1, Pallas kernels, body(): pl.pallas_call(functools.partial(kernel, groups, levels), out_shape=jax.S...  59.8 us
    unnamed x11, local copies, waits for them, and re-layouts  2.82 us
    transpose x1, local copies, waits for them, and re-layouts, body(): return out.transpose(1, 0, 2)  1.65 us

profile of v2, /device:TPU:17, one launch (start us, length us, event | category | flops | bytes accessed | tf_op | source)
XLA Modules:
  0.0 65.5 jit_solution(17866328523657340972)
XLA Ops:
  0.7 0.1 iota_add_fusion
  0.7 0.0 copy-start.3
  0.8 0.1 add.52
  0.8 0.6 copy-done.3
  1.4 0.2 and_reduce_fusion
  1.6 0.0 copy-start.2
  1.6 0.7 %copy-done.2 = s32[256]{0:T(256)S(1)} copy-done((s32[256]{0:T(256)S(1)}, s32[256]{0:T(256)}, u32[]{:S(2)}) %copy-start.2) | copy-done | bytes 1048
  2.3 0.0 copy-start.1
  2.3 0.1 subtract_select_fusion.rel_ref
  2.3 0.0 copy-start
  2.4 1.1 %copy.22 = bf16[128,8,128]{2,0,1:T(8,128)(2,1)S(1)} copy(bf16[128,8,128]{2,1,0:T(8,128)(2,1)} %param.7) | data formatting | bytes 524288 | tf_op args[1]
  3.4 0.0 copy-done.1
  3.4 0.2 copy.17
  3.7 0.1 pad_maximum_fusion.kv_ref
  3.7 0.0 copy-done
  3.7 0.3 copy.21
  4.0 59.8 %shard_map.64 = bf16[16,256,128]{2,1,0:T(8,128)(2,1)S(1)} custom-call(s32[24,256]{1,0:T(8,128)S(1)} %subtract_select_fusion.rel_ref, bf16[16,256,128]{2,1,0:T(8,128)(2,1)S(1)} %bitcast.16, bf16[8,2,128,128]{3,2,1,0:T(8,128)(2,1)S(1)} %pad_maximum_fusion.kv_ref), custom_call_target="tpu_custom_call" | custom-call | tf_op jit(solution)/shard_map/pallas_call | solution.py:240
  63.8 1.6 %copy.18 = bf16[256,16,128]{2,1,0:T(8,128)(2,1)} copy(bf16[256,16,128]{2,0,1:T(8,128)(2,1)S(1)} %bitcast.15) | data formatting | bytes 2097152 | tf_op jit(solution)/shard_map/transpose | solution.py:259
  (3 shorter events, 0.0 us)
Async XLA Ops:
  0.7 0.7 %copy-start.3 = (s32[1,18]{1,0:T(1,128)S(1)}, s32[1,18]{1,0:T(1,128)}, u32[]{:S(2)}) copy-start(s32[1,18]{1,0:T(1,128)} %param.10) | copy-start | bytes 220
  1.6 0.7 %copy-start.2 = (s32[256]{0:T(256)S(1)}, s32[256]{0:T(256)}, u32[]{:S(2)}) copy-start(s32[256]{0:T(256)} %param.9) | copy-start | bytes 3076
  2.3 1.2 %copy-start.1 = (bf16[128,8,128]{2,1,0:T(8,128)(2,1)S(1)}, bf16[128,8,128]{2,1,0:T(8,128)(2,1)}, u32[]{:S(2)}) copy-start(bf16[128,8,128]{2,1,0:T(8,128)(2,1)} %param.8) | copy-start | bytes 786436
  2.3 1.4 %copy-start = (bf16[256,16,128]{2,1,0:T(8,128)(2,1)S(1)}, bf16[256,16,128]{2,1,0:T(8,128)(2,1)}, u32[]{:S(2)}) copy-start(bf16[256,16,128]{2,1,0:T(8,128)(2,1)} %param.6) | copy-start | bytes 3145732
